TPU v7x, 32 devices: a 4x4x1 block of a 4x4x8 slice. The times are simulated.
32 devices in a mesh: data: 1 (over z), tp2: 4 (over y), tp: 8 (over x, core).
Axes of the slice: x: 4, y: 4, z: 1, core: 2. Of those that a mesh axis runs over, the one named last changes fastest.
The devices are a block of a 4x4x8 slice.
Arguments:
- x_resid: bfloat16 [4096, 8192], P(('data', 'tp'), 'tp2')
- ln_scale: float32 [8192], P('tp2')
- w_in: bfloat16 [8192, 28672], P('tp2', 'tp')
- w_out: bfloat16 [28672, 8192], P('tp', 'tp2')
Outputs:
- output: bfloat16 [4096, 8192], P(('data', 'tp'), 'tp2')
All inputs are finite; a program needn't handle non-finite values.
Results may differ from a plain program's by a relative error of at most 0.00132.
Values are sent between devices in bfloat16 or wider.
A program may use at most 768 MiB of HBM per device.

v0:
```python
import jax
import jax.numpy as jnp
from jax import lax
from jax.sharding import PartitionSpec as P

LN_EPS = 1e-6


def solution(mesh):
    tp2_size = mesh.shape["tp2"]
    row_spec = P(("data", "tp"), "tp2")

    def local_block(x_loc, scale_loc, w_in_loc, w_out_loc):
        x_f32 = x_loc.astype(jnp.float32)
        model_dim = x_f32.shape[1] * tp2_size
        row_stats = jnp.stack([jnp.sum(x_f32, axis=1), jnp.sum(x_f32 * x_f32, axis=1)], axis=1)
        row_stats = lax.psum(row_stats, "tp2")
        row_mean = row_stats[:, 0:1] / model_dim
        row_var = row_stats[:, 1:2] / model_dim - row_mean * row_mean
        x_norm = ((x_f32 - row_mean) * lax.rsqrt(row_var + LN_EPS) * scale_loc).astype(jnp.bfloat16)
        x_group = lax.all_gather(x_norm, "tp", axis=0, tiled=True)
        part_pre = jnp.dot(x_group, w_in_loc, preferred_element_type=jnp.float32)
        pre_act = lax.psum_scatter(part_pre, "tp2", scatter_dimension=0, tiled=True)
        hidden = jax.nn.gelu(pre_act, approximate=True).astype(jnp.bfloat16)
        hidden_all = lax.all_gather(hidden, "tp2", axis=0, tiled=True)
        part_out = jnp.dot(hidden_all, w_out_loc, preferred_element_type=jnp.float32)
        mlp_out = lax.psum_scatter(part_out, "tp", scatter_dimension=0, tiled=True)
        return (x_f32 + mlp_out).astype(jnp.bfloat16)

    return jax.shard_map(local_block, mesh=mesh, in_specs=(row_spec, P("tp2"), P("tp2", "tp"), P("tp", "tp2")), out_specs=row_spec, check_vma=False)
```

profile of v0, /device:TPU:97, one launch (start us, length us, event | category | flops | bytes accessed | tf_op | source)
XLA Modules:
  0.0 1179.5 jit_solution(6899801438375404804)
XLA Ops:
  6.5 0.0 all-gather.3.cloned.1.call-start
  6.6 2.3 convert_reduce_fusion
  8.9 11.2 psum.7
  20.1 3.6 fusion.11
  23.7 0.1 all-gather.3.cloned.1.call-update
  23.8 0.1 reduce-scatter.3.cloned.1.call-start
  23.9 84.4 %all-gather.3.cloned.1.call-done = bf16[4096,2048]{1,0:T(8,128)(2,1)} async-done(((bf16[512,2048]{1,0:T(8,128)(2,1)}), bf16[4096,2048]{1,0:T(8,128)(2,1)}) %all-gather.3.cloned.1.call-update) | async-done | bytes 16777232 | tf_op jit(solution)/shard_map/all_gather | solution.py:21
  108.3 71.2 %fusion.14 = f32[4096,3584]{1,0:T(8,128)} fusion(bf16[4096,2048]{1,0:T(8,128)(2,1)} %all-gather.3.cloned.1.call-done, bf16[2048,3584]{1,0:T(8,128)(2,1)} %param.6), kind=kOutput, calls=%fused_computation.23 | convolution fusion | flops 60129542144 | bytes 90177536 | tf_op jit(solution)/shard_map/dot_general | solution.py:22
  179.4 0.1 reduce-scatter.3.cloned.1.call-update
  179.5 0.2 all-gather.5.cloned.1.call-start
  179.7 482.8 %reduce-scatter.3.cloned.1.call-done = f32[1024,3584]{1,0:T(8,128)} async-done(((f32[4096,3584]{1,0:T(8,128)}), f32[1024,3584]{1,0:T(8,128)}) %reduce-scatter.3.cloned.1.call-update) | async-done | bytes 14680080 | tf_op jit(solution)/shard_map/reduce_scatter | solution.py:23
  662.5 10.1 fusion.7
  672.6 0.1 all-gather.5.cloned.1.call-update
  672.6 0.1 reduce-scatter.5.cloned.1.call-start
  672.7 256.5 %all-gather.5.cloned.1.call-done = bf16[4096,3584]{1,0:T(8,128)(2,1)} async-done(((bf16[1024,3584]{1,0:T(8,128)(2,1)}), bf16[4096,3584]{1,0:T(8,128)(2,1)}) %all-gather.5.cloned.1.call-update) | async-done | bytes 29360144 | tf_op jit(solution)/shard_map/all_gather | solution.py:25
  929.2 70.7 %fusion.15 = f32[4096,2048]{1,0:T(8,128)} fusion(bf16[4096,3584]{1,0:T(8,128)(2,1)} %all-gather.5.cloned.1.call-done, bf16[3584,2048]{1,0:T(8,128)(2,1)} %param.7), kind=kOutput, calls=%fused_computation.24 | convolution fusion | flops 60129542144 | bytes 77594624 | tf_op jit(solution)/shard_map/dot_general | solution.py:26
  999.9 0.0 copy-start
  999.9 0.1 reduce-scatter.5.cloned.1.call-update
  999.9 168.8 %reduce-scatter.5.cloned.1.call-done = f32[512,2048]{1,0:T(8,128)} async-done(((f32[4096,2048]{1,0:T(8,128)}), f32[512,2048]{1,0:T(8,128)}) %reduce-scatter.5.cloned.1.call-update) | async-done | bytes 4194320 | tf_op jit(solution)/shard_map/reduce_scatter | solution.py:27
  1168.8 0.0 copy-done
  1168.8 4.2 fusion.12
  (2 shorter events, 0.0 us)
Async XLA Ops:
  6.5 101.7 %all-gather.3.cloned.1.call-start = ((), (), s32[]{:S(2)}) async-start(), calls=%async_computation.2 | async-start | bytes 18874368 | tf_op jit(solution)/shard_map/all_gather | solution.py:21
  23.8 638.7 %reduce-scatter.3.cloned.1.call-start = ((), (), s32[]{:S(2)}) async-start(), calls=%async_computation.3 | async-start | bytes 73400320 | tf_op jit(solution)/shard_map/reduce_scatter | solution.py:23
  179.5 749.7 %all-gather.5.cloned.1.call-start = ((), (), s32[]{:S(2)}) async-start(), calls=%async_computation.4 | async-start | bytes 36700160 | tf_op jit(solution)/shard_map/all_gather | solution.py:25
  672.6 496.1 %reduce-scatter.5.cloned.1.call-start = ((), (), s32[]{:S(2)}) async-start(), calls=%async_computation.5 | async-start | bytes 37748736 | tf_op jit(solution)/shard_map/reduce_scatter | solution.py:27
  999.9 168.9 %copy-start = (bf16[512,2048]{1,0:T(8,128)(2,1)S(1)}, bf16[512,2048]{1,0:T(8,128)(2,1)}, u32[]{:S(2)}) copy-start(bf16[512,2048]{1,0:T(8,128)(2,1)} %param.4) | copy-start | bytes 6291460
Sparse Core Ops, SparseCore 0:
  23.9 84.3 all-gather.2
  179.6 482.8 reduce-scatter.2
  672.8 256.3 all-gather.4
  1000.0 168.6 reduce-scatter.4
where the time goes:
time: 1180 us
  waiting for transfers between devices  993 us (84%)
  matrix products  142 us (12%)
  other arithmetic  20.2 us (2%)
  between operations  13.2 us (1%)
    reduce_scatter x1, waiting for transfers between devices, local_block(): pre_act = lax.psum_scatter(part_pre, 'tp2', scatter_dimension=0, tiled=True)  483 us
    all_gather x1, waiting for transfers between devices, local_block(): hidden_all = lax.all_gather(hidden, 'tp2', axis=0, tiled=True)  256 us
    reduce_scatter x1, waiting for transfers between devices, local_block(): mlp_out = lax.psum_scatter(part_out, 'tp', scatter_dimension=0, tiled=True)  169 us
    all_gather x1, waiting for transfers between devices, local_block(): x_group = lax.all_gather(x_norm, 'tp', axis=0, tiled=True)  84.4 us
    dot_general x1, matrix products, local_block(): part_pre = jnp.dot(x_group, w_in_loc, preferred_element_type=jnp.float32)  71.2 us
    dot_general x1, matrix products, local_block(): jnp.dot(hidden_all, w_out_loc, preferred_element_type=jnp.float32)  70.7 us
  transfers between devices with their start and end apart: 4, of which 4 were waited for; matrix products, arithmetic and copies ran while one was open for 0% of the time, Pallas kernels for 0%

commit v1 on v0

v1 whole, which is shorter than its diff:
```python
import functools

import jax
import jax.numpy as jnp
from jax import lax
from jax.experimental import pallas as pl
from jax.experimental.pallas import tpu as pltpu
from jax.sharding import PartitionSpec as P

LN_EPS = 1e-6
RING = 4
TICKS = 16
AHEAD = 4
HSLOTS = 5
MESH = pl.DeviceIdType.MESH
BF16, F32 = jnp.bfloat16, jnp.float32


def kernel(dims, x_ref, g_ref, w1_ref, w2_ref, y_ref, raw_ref, xall_ref, w1v, w2v, xv, hv, sv, pv, pr, hr, tr, xr, gv, lr, ln,
           g_s, g_r, raw_s, raw_r, w1_s, w1_r, x_s, x_r, d_s, d_r, h_s, h_r, q_s, p_s, p_r, f_s, f_r, t_s, t_r, l_s, xl_s, o_s):
    T, KB, NS, DB, r, M = dims
    J = TICKS
    K = RING * KB
    half = r // 2
    d = lax.axis_index("data")
    y = lax.axis_index("tp2")
    tp = lax.axis_index("tp")
    x, c = tp // 2, tp % 2
    yp, yo, ym = (y + 1) % RING, (y + 2) % RING, (y + 3) % RING
    xp, xo, xm = (x + 1) % RING, (x + 2) % RING, (x + 3) % RING
    to_yp, to_ym, to_yo = (d, yp, tp), (d, ym, tp), (d, yo, tp)
    to_xp, to_xm = (d, y, xp * 2 + c), (d, y, xm * 2 + c)
    to_pt = (d, y, x * 2 + 1 - c)

    def rc(src, dst, ss, rs, dev):
        return pltpu.make_async_remote_copy(src_ref=src, dst_ref=dst, send_sem=ss, recv_sem=rs, device_id=dev, device_id_type=MESH)

    def loop(lo, hi, f):
        def body(i, carry):
            f(i)
            return carry
        lax.fori_loop(lo, hi, body, 0)

    barrier = pltpu.get_barrier_semaphore()
    for dev in (to_yp, to_ym, to_yo, to_xp, to_xm, to_pt):
        pl.semaphore_signal(barrier, inc=1, device_id=dev, device_id_type=MESH)
    pl.semaphore_wait(barrier, 6)

    def raw_own(j, dev, i, k):
        rows = pl.ds(pl.multiple_of(j * r, r), r)
        return rc(x_ref.at[rows], raw_ref.at[y, rows], raw_s.at[i], raw_r.at[j, k], dev)

    def raw_block(j, b):
        return raw_ref.at[b, pl.ds(pl.multiple_of(j * r, r), r)]

    def raw_relay(j, b, off, dev, i):
        part = raw_ref.at[b, pl.ds(pl.multiple_of(j * r + off, half), half)]
        return rc(part, part, raw_s.at[i], raw_r.at[j, 2], dev)

    def raw_wait(j, b, k):
        rc(raw_block(j, b), raw_block(j, b), raw_s.at[0], raw_r.at[j, k], to_yp).wait_recv()

    gammas = [rc(g_ref, gv.at[y], g_s.at[i], g_r.at[k], dev) for i, (dev, k) in enumerate(((to_yp, 1), (to_ym, 0), (to_yo, 2)))]
    for cp in gammas:
        cp.start()
    raw_own(0, to_yp, 0, 1).start()
    raw_own(0, to_ym, 1, 0).start()
    raw_own(0, to_yo, 4, 2).start()

    def send_raw(j):
        raw_own(j, to_yp, 0, 1).start()
        raw_own(j, to_ym, 1, 0).start()
    loop(1, J, send_raw)

    def w1_copy(b, dev, i, k):
        return rc(w1_ref.at[:, pl.ds(pl.multiple_of(b * NS, 128), NS)], w1v.at[pl.ds(pl.multiple_of(y * KB, KB), KB)], w1_s.at[i], w1_r.at[k], dev)

    own_g = pltpu.make_async_copy(g_ref, gv.at[y], l_s.at[3])
    own_x = pltpu.make_async_copy(x_ref, xr, l_s.at[4])
    own_w1 = pltpu.make_async_copy(w1_ref.at[:, pl.ds(pl.multiple_of(y * NS, 128), NS)], w1v.at[pl.ds(pl.multiple_of(y * KB, KB), KB)], l_s.at[5])
    own_w2 = pltpu.make_async_copy(w2_ref, w2v, l_s.at[6])
    own_g.start()
    own_x.start()
    own_w1.start()
    own_w2.start()

    def xrow(j, b):
        return pl.multiple_of((j * 8 + b) * r, r)

    def x_own(j, dev, i, k):
        blk = xall_ref.at[pl.ds(xrow(j, x), r)]
        return rc(blk, blk, x_s.at[i], x_r.at[j, k], dev)

    def x_relay(j, b, off, dev, i):
        blk = xall_ref.at[pl.ds(pl.multiple_of(xrow(j, b) + off, half), half)]
        return rc(blk, blk, x_s.at[i], x_r.at[j, 2], dev)

    def x_wait(j, b, k):
        blk = xall_ref.at[pl.ds(xrow(j, b), r)]
        rc(blk, blk, x_s.at[0], x_r.at[j, k], to_xp).wait_recv()

    def d_copy(j, b, i):
        return rc(xall_ref.at[pl.ds(xrow(j, b), r)], xall_ref.at[pl.ds(xrow(j, 4 + b), r)], d_s.at[i], d_r.at[j, i], to_pt)

    def d_wait(j, b, i):
        blk = xall_ref.at[pl.ds(xrow(j, 4 + b), r)]
        rc(blk, blk, d_s.at[i], d_r.at[j, i], to_pt).wait_recv()

    def norm(j):
        raw_wait(j, yo, 2)
        loads = [pltpu.make_async_copy(raw_block(j, b), lr.at[i], l_s.at[i]) for i, b in enumerate((yp, ym, yo))]
        for cp in loads:
            cp.start()
        for cp in loads:
            cp.wait()
        rows = pl.ds(pl.multiple_of(j * r, r), r)
        parts = [(y, lambda: xr[rows]), (yp, lambda: lr[0]), (ym, lambda: lr[1]), (yo, lambda: lr[2])]
        total = jnp.zeros((r, 1), F32)
        for _, get in parts:
            total += jnp.sum(get().astype(F32), axis=1, keepdims=True)
        mean = total / K
        total = jnp.zeros((r, 1), F32)
        for _, get in parts:
            dev = get().astype(F32) - mean
            total += jnp.sum(dev * dev, axis=1, keepdims=True)
        inv = lax.rsqrt(total / K + LN_EPS)
        for b, get in parts:
            ln[:, pl.ds(pl.multiple_of(b * KB, KB), KB)] = ((get().astype(F32) - mean) * inv * gv[b]).astype(BF16)
        out = pltpu.make_async_copy(ln, xall_ref.at[pl.ds(xrow(j, x), r)], l_s.at[7])
        out.start()
        out.wait()
        x_own(j, to_xp, 0, 1).start()
        x_own(j, to_xm, 1, 0).start()
        d_copy(j, x, 0).start()

    def x_step(j):
        x_wait(j, xp, 0)
        x_wait(j, xm, 1)
        x_relay(j, xm, 0, to_xp, 2).start()
        x_relay(j, xp, half, to_xm, 3).start()
        d_copy(j, xp, 1).start()
        d_copy(j, xm, 2).start()

    def x_last(j):
        x_wait(j, xo, 2)
        d_copy(j, xo, 3).start()

    own_x.wait()
    own_g.wait()
    for b, k in ((yp, 0), (ym, 1), (yo, 2)):
        rc(gv.at[b], gv.at[b], g_s.at[0], g_r.at[k], to_yp).wait_recv()
    raw_wait(0, yp, 0)
    raw_wait(0, ym, 1)
    norm(0)

    def raw_step(j):
        raw_wait(j, yp, 0)
        raw_wait(j, ym, 1)
        raw_relay(j, ym, 0, to_yp, 2).start()
        raw_relay(j, yp, half, to_ym, 3).start()
    loop(1, J, raw_step)

    w1_sends = [w1_copy(b, dev, i, k) for i, (b, dev, k) in enumerate(((yp, to_yp, 1), (ym, to_ym, 0), (yo, to_yo, 2)))]
    for cp in w1_sends:
        cp.start()

    def norm_step(j):
        norm(j)

        @pl.when(j >= AHEAD)
        def _():
            x_step(j - AHEAD)

        @pl.when(j >= AHEAD + 2)
        def _():
            x_last(j - AHEAD - 2)
    loop(1, J, norm_step)

    def x_load(t):
        return pltpu.make_async_copy(xall_ref.at[pl.ds(pl.multiple_of(t * M, M), M)], xv.at[t % 2], xl_s.at[t % 2])

    def x_fetch(t):
        for i, b in enumerate((x, xp, xm, xo)):
            d_wait(t, b, i)
        x_load(t).start()

    x_fetch(0)
    own_w1.wait()
    own_w2.wait()
    for b, k in ((yp, 0), (ym, 1), (yo, 2)):
        blk = w1v.at[pl.ds(pl.multiple_of(b * KB, KB), KB)]
        rc(blk, blk, w1_s.at[0], w1_r.at[k], to_yp).wait_recv()

    def hcols(b):
        return pl.ds(pl.multiple_of(b * NS, 128), NS)

    def h_own(t, dev, i, k):
        blk = hv.at[t % HSLOTS, :, hcols(y)]
        return rc(blk, blk, h_s.at[t % HSLOTS, i], h_r.at[t, k], dev)

    def h_relay(t, b, off, dev, i):
        blk = hv.at[t % HSLOTS, pl.ds(off, M // 2), hcols(b)]
        return rc(blk, blk, q_s.at[t % HSLOTS, i], h_r.at[t, 2], dev)

    def h_wait(t, b, k):
        blk = hv.at[t % HSLOTS, :, hcols(b)]
        rc(blk, blk, h_s.at[0, 0], h_r.at[t, k], to_yp).wait_recv()

    def first(t):
        cut = NS * 4 // 7
        for lo, hi in ((0, cut), (cut, NS)):
            u = jnp.dot(xv[t % 2], w1v[:, lo:hi], preferred_element_type=F32)
            hv[t % HSLOTS, :, pl.ds(pl.multiple_of(y * NS + lo, 128), hi - lo)] = jax.nn.gelu(u, approximate=True).astype(BF16)

    def p_copy(j):
        return rc(pv.at[j % 2], pr.at[j % 2], p_s.at[j % 2], p_r.at[j], to_pt)

    def second(j):
        tn = DB // 2

        def cols(n):
            o = pl.ds(pl.multiple_of(n * tn, tn), tn)
            u = jnp.dot(hv[j % HSLOTS], w2v[:, o], preferred_element_type=F32)
            sv[j % 4, :, o] = u[:M // 2]
            pv[j % 2, :, o] = u[M // 2:]
        loop(0, 2, cols)

    def srow(b):
        return pl.multiple_of(b * r, r)

    def f_copy(j, off, dev, i, k):
        return rc(sv.at[j % 4, pl.ds(pl.multiple_of(srow(xo) + off, half), half)], hr.at[j % 2, k], f_s.at[j % 4, i], f_r.at[j, k], dev)

    def t_copy(j, b, dev, i, k):
        return rc(sv.at[j % 4, pl.ds(srow(b), r)], tr.at[j % 2, k], t_s.at[j % 4, i], t_r.at[j, k], dev)

    def add_partner(j):
        p_copy(j).wait_recv()
        sv[j % 4] += pr[j % 2]
        f_copy(j, 0, to_xp, 0, 1).start()
        f_copy(j, half, to_xm, 1, 0).start()

    def add_far(j):
        f_copy(j, 0, to_xp, 0, 1).wait_recv()
        f_copy(j, half, to_xm, 1, 0).wait_recv()
        sv[j % 4, pl.ds(srow(xp), half)] += hr[j % 2, 1]
        sv[j % 4, pl.ds(pl.multiple_of(srow(xm) + half, half), half)] += hr[j % 2, 0]
        t_copy(j, xp, to_xp, 0, 1).start()
        t_copy(j, xm, to_xm, 1, 0).start()

    def out_copy(j):
        rows = pl.ds(pl.multiple_of(j * r, r), r)
        return pltpu.make_async_copy(xr.at[rows], y_ref.at[rows], o_s)

    def finish(j):
        t_copy(j, xp, to_xp, 0, 1).wait_recv()
        t_copy(j, xm, to_xm, 1, 0).wait_recv()
        rows = pl.ds(pl.multiple_of(j * r, r), r)
        mlp = sv[j % 4, pl.ds(srow(x), r)] + tr[j % 2, 0] + tr[j % 2, 1]
        xr[rows] = (xr[rows].astype(F32) + mlp).astype(BF16)
        out_copy(j).start()

    def tick(t):
        def when(lag, f, hi=J):
            @pl.when(jnp.logical_and(t >= lag, t < hi + lag))
            def _():
                f(t - lag)

        def sent(j):
            h_own(j, to_yp, 0, 1).wait_send()
            h_own(j, to_ym, 1, 0).wait_send()
            h_relay(j, ym, 0, to_yp, 0).wait_send()
            h_relay(j, yp, M // 2, to_ym, 1).wait_send()
        when(3, sent)

        def start(j):
            x_load(j).wait()

            @pl.when(j + 1 < J)
            def _():
                x_fetch(j + 1)
            first(j)
            h_own(j, to_yp, 0, 1).start()
            h_own(j, to_ym, 1, 0).start()
        when(0, start)

        def relay(j):
            h_wait(j, yp, 0)
            h_wait(j, ym, 1)
            h_relay(j, ym, 0, to_yp, 0).start()
            h_relay(j, yp, M // 2, to_ym, 1).start()
        when(1, relay)
        when(5, finish)
        when(4, add_far)
        when(3, add_partner)

        def rest_step(j):
            x_step(j + J - AHEAD)
        when(2, rest_step, AHEAD)

        def rest_last(j):
            x_last(j + J - AHEAD - 2)
        when(2, rest_last, AHEAD + 2)

        def p_sent(j):
            p_copy(j).wait_send()
        when(4, p_sent)

        def out(j):
            h_wait(j, yo, 2)
            second(j)
            p_copy(j).start()
        when(2, out)

        def s_sent(j):
            f_copy(j, 0, to_xp, 0, 1).wait_send()
            f_copy(j, half, to_xm, 1, 0).wait_send()
            t_copy(j, xp, to_xp, 0, 1).wait_send()
            t_copy(j, xm, to_xm, 1, 0).wait_send()
        when(5, s_sent)
    loop(0, J + 5, tick)

    for cp in gammas + w1_sends:
        cp.wait_send()

    def drain(src, ss):
        rc(src, src, ss, raw_r.at[0, 0], to_yp).wait_send()
    drain(x_ref, raw_s.at[0])
    drain(x_ref, raw_s.at[1])
    rest = T // J * (J - 1) // 2
    drain(x_ref.at[pl.ds(0, rest)], raw_s.at[2])
    drain(x_ref.at[pl.ds(0, rest)], raw_s.at[3])
    drain(x_ref.at[pl.ds(0, r)], raw_s.at[4])
    for i in (0, 1):
        drain(xall_ref.at[pl.ds(0, T)], x_s.at[i])
    for i in (2, 3):
        drain(xall_ref.at[pl.ds(0, T // 2)], x_s.at[i])
    for i in range(4):
        drain(xall_ref.at[pl.ds(0, T)], d_s.at[i])
    pltpu.make_async_copy(xr, y_ref, o_s).wait()


def solution(mesh):
    assert mesh.shape["tp2"] == RING and mesh.shape["tp"] == 2 * RING
    row_spec = P(("data", "tp"), "tp2")

    def local_block(x_loc, scale_loc, w_in_loc, w_out_loc):
        T, KB = x_loc.shape
        NB, DB = w_out_loc.shape
        NS = NB // RING
        r = T // TICKS
        M = 8 * r
        K = RING * KB
        J = TICKS
        dma = pltpu.SemaphoreType.DMA
        any_spec = pl.BlockSpec(memory_space=pl.ANY)
        outs = pl.pallas_call(
            functools.partial(kernel, (T, KB, NS, DB, r, M)),
            out_shape=[
                jax.ShapeDtypeStruct((T, DB), BF16),
                jax.ShapeDtypeStruct((RING, T, KB), BF16),
                jax.ShapeDtypeStruct((J * M, K), BF16),
            ],
            in_specs=[any_spec] * 4,
            out_specs=[any_spec] * 3,
            scratch_shapes=[
                pltpu.VMEM((K, NS), BF16),
                pltpu.VMEM((NB, DB), BF16),
                pltpu.VMEM((2, M, K), BF16),
                pltpu.VMEM((HSLOTS, M, NB), BF16),
                pltpu.VMEM((4, M // 2, DB), F32),
                pltpu.VMEM((2, M // 2, DB), F32),
                pltpu.VMEM((2, M // 2, DB), F32),
                pltpu.VMEM((2, 2, r // 2, DB), F32),
                pltpu.VMEM((2, 2, r, DB), F32),
                pltpu.VMEM((T, DB), BF16),
                pltpu.VMEM((RING, 1, KB), F32),
                pltpu.VMEM((3, r, KB), BF16),
                pltpu.VMEM((r, K), BF16),
                dma((3,)), dma((3,)),
                dma((5,)), dma((J, 3)),
                dma((3,)), dma((3,)),
                dma((4,)), dma((J, 3)),
                dma((4,)), dma((J, 4)),
                dma((HSLOTS, 2)), dma((J, 3)), dma((HSLOTS, 2)),
                dma((2,)), dma((J,)),
                dma((4, 2)), dma((J, 2)),
                dma((4, 2)), dma((J, 2)),
                dma((8,)), dma((2,)), dma,
            ],
            compiler_params=pltpu.CompilerParams(collective_id=0, has_side_effects=True, vmem_limit_bytes=67043328),
        )(x_loc, scale_loc.reshape(1, KB), w_in_loc, w_out_loc)
        return outs[0]

    return jax.shard_map(local_block, mesh=mesh, in_specs=(row_spec, P("tp2"), P("tp2", "tp"), P("tp", "tp2")), out_specs=row_spec, check_vma=False)
```

time: 1180 us -> 543 us (0.46)
  waiting for transfers between devices: 993 us -> 0 us
  Pallas kernels: 0 us -> 536 us
  matrix products: 142 us -> 0 us
  other arithmetic: 20.2 us -> 0 us
  between operations: 13.2 us -> 0.01 us
    reduce_scatter x2 -> x0, waiting for transfers between devices: 652 us -> none  [the longest x1 483 us: local_block(): pre_act = lax.psum_scatter(part_pre, 'tp2', scatter_dimension=0, tiled=True)]
    pallas_call x0 -> x1, Pallas kernels: none -> 536 us  [local_block(): pl.pallas_call(functools.partial(kernel, (T, KB, NS, DB, r, M)), out_shap...]
    all_gather x2 -> x0, waiting for transfers between devices: 341 us -> none  [the longest x1 256 us: local_block(): hidden_all = lax.all_gather(hidden, 'tp2', axis=0, tiled=True)]
    dot_general x2 -> x0, matrix products: 142 us -> none  [the longest x1 71.2 us: local_block(): part_pre = jnp.dot(x_group, w_in_loc, preferred_element_type=jnp.float32)]
    convert_element_type x3 -> x0, other arithmetic: 17.9 us -> none  [the longest x1 10.1 us: local_block(): hidden = jax.nn.gelu(pre_act, approximate=True).astype(jnp.bfloat16)]
  transfers between devices with their start and end apart: 4 -> 0, of which waited for: 4 -> 0; matrix products, arithmetic and copies ran while one was open for 0% -> 0% of each run, Pallas kernels for 0% -> 0%
where the time goes in v1:
time: 543 us; the launch traced here: 539 us
  Pallas kernels  536 us (99%)
    pallas_call x1, Pallas kernels, local_block(): pl.pallas_call(functools.partial(kernel, (T, KB, NS, DB, r, M)), out_shap...  536 us

profile of v1, /device:TPU:97, one launch (start us, length us, event | category | flops | bytes accessed | tf_op | source)
XLA Modules:
  0.0 539.0 jit_solution(11462125105035260153)
XLA Ops:
  0.0 535.8 %shard_map.46 = (bf16[512,2048]{1,0:T(8,128)(2,1)}, bf16[4,512,2048]{2,1,0:T(8,128)(2,1)}, bf16[4096,8192]{1,0:T(8,128)(2,1)}) custom-call(bf16[512,2048]{1,0:T(8,128)(2,1)} %x_ref.1, f32[1,2048]{1,0:T(1,128)} %bitcast.1, bf16[2048,3584]{1,0:T(8,128)(2,1)} %w1_ref.1, bf16[3584,2048]{1,0:T(8,128)(2,1)} %w2_ref.1), custom_call_target="tpu_custom_call" | custom-call | tf_op jit(solution)/shard_map/pallas_call | solution.py:357
  535.8 3.2 copy.6

commit v2 on v0

v2 whole, which is shorter than its diff:
```python
import functools

import jax
import jax.numpy as jnp
from jax import lax
from jax.experimental import pallas as pl
from jax.experimental.pallas import tpu as pltpu
from jax.sharding import PartitionSpec as P

LN_EPS = 1e-6
RING = 4
CHUNKS = 16
FULL = 14
SPLIT = 2
TICKS = FULL + (CHUNKS - FULL) * SPLIT
AHEAD = 4
CATCH = 8
RSLOTS, HSLOTS, SSLOTS, VSLOTS, FSLOTS = 8, 5, 4, 3, 4
MESH = pl.DeviceIdType.MESH
BF16, F32 = jnp.bfloat16, jnp.float32


def kernel(dims, x_ref, g_ref, w1_ref, w2_ref, y_ref, raw_ref, xall_ref, w1v, w2v, xv, hv, sv, pv, pr, hr, tr, xr, gv, lr, ln,
           g_s, g_r, raw_s, raw_r, w1_s, w1_r, x_s, x_r, d_s, d_r, h_s, h_r, q_s, p_s, p_r, f_s, f_r, t_s, t_r, l_s, xl_s, o_s):
    T, KB, NS, DB, r = dims
    J, K, small = CHUNKS, RING * KB, r // SPLIT
    half = r // 2
    d = lax.axis_index("data")
    y = lax.axis_index("tp2")
    tp = lax.axis_index("tp")
    x, c = tp // 2, tp % 2
    yp, yo, ym = (y + 1) % RING, (y + 2) % RING, (y + 3) % RING
    xp, xo, xm = (x + 1) % RING, (x + 2) % RING, (x + 3) % RING
    to_yp, to_ym, to_yo = (d, yp, tp), (d, ym, tp), (d, yo, tp)
    to_xp, to_xm = (d, y, xp * 2 + c), (d, y, xm * 2 + c)
    to_pt = (d, y, x * 2 + 1 - c)

    def rc(src, dst, ss, rs, dev):
        return pltpu.make_async_remote_copy(src_ref=src, dst_ref=dst, send_sem=ss, recv_sem=rs, device_id=dev, device_id_type=MESH)

    def arrived(ref, sem):
        rc(ref, ref, o_s, sem, to_pt).wait_recv()

    def left(ref, sem):
        rc(ref, ref, sem, o_s, to_pt).wait_send()

    def loop(lo, hi, f):
        def body(i, carry):
            f(i)
            return carry
        lax.fori_loop(lo, hi, body, 0)

    barrier = pltpu.get_barrier_semaphore()
    for dev in (to_yp, to_ym, to_yo, to_xp, to_xm, to_pt):
        pl.semaphore_signal(barrier, inc=1, device_id=dev, device_id_type=MESH)
    pl.semaphore_wait(barrier, 6)

    def raw_block(j, b):
        return raw_ref.at[b, pl.ds(pl.multiple_of(j * r, r), r)]

    def raw_own(j, dev, i, k=0):
        rows = pl.ds(pl.multiple_of(j * r, r), r)
        return rc(x_ref.at[rows], raw_ref.at[y, rows], raw_s.at[i], raw_r.at[j % RSLOTS, k], dev)

    def raw_relay(j, b, off, dev, i):
        part = raw_ref.at[b, pl.ds(pl.multiple_of(j * r + off, half), half)]
        return rc(part, part, raw_s.at[i], raw_r.at[j % RSLOTS, 1], dev)

    def send_raw(j):
        raw_own(j, to_yp, 0).start()
        raw_own(j, to_ym, 1).start()

    send_raw(0)
    raw_own(0, to_yo, 4, 1).start()
    gammas = [rc(g_ref, gv.at[y], g_s, g_r, dev) for dev in (to_yp, to_ym, to_yo)]
    for cp in gammas:
        cp.start()
    for j in range(1, AHEAD):
        send_raw(j)

    cut = NS * 4 // 7
    parts = ((0, cut), (cut, NS))

    def w1_block(b, part):
        lo, hi = parts[part]
        return w1v.at[pl.ds(pl.multiple_of(b * KB, KB), KB), pl.ds(lo, hi - lo)]

    def w1_copy(b, dev, part):
        lo, hi = parts[part]
        cols = w1_ref.at[:, pl.ds(pl.multiple_of(b * NS + lo, 128), hi - lo)]
        return rc(cols, w1_block(y, part), w1_s.at[part], w1_r.at[part], dev)

    def w1_wait(part):
        lo, hi = parts[part]
        arrived(w1v.at[pl.ds(0, 3 * KB), pl.ds(lo, hi - lo)], w1_r.at[part])

    own_g = pltpu.make_async_copy(g_ref, gv.at[y], l_s.at[3])
    own_x = pltpu.make_async_copy(x_ref, xr, l_s.at[4])
    own_w1 = pltpu.make_async_copy(w1_ref.at[:, pl.ds(pl.multiple_of(y * NS, 128), NS)], w1v.at[pl.ds(pl.multiple_of(y * KB, KB), KB)], l_s.at[5])
    own_w2 = pltpu.make_async_copy(w2_ref, w2v, l_s.at[6])
    own_g.start()
    own_x.start()
    own_w1.start()
    own_w2.start()

    def x_own(j, dev, i):
        return rc(xall_ref.at[j, x], xall_ref.at[j, x], x_s.at[i], x_r.at[j, 0], dev)

    def x_relay(j, b, off, dev, i):
        blk = xall_ref.at[j, b, pl.ds(off, half)]
        return rc(blk, blk, x_s.at[i], x_r.at[j, 1], dev)

    def d_copy(j, b, i):
        return rc(xall_ref.at[j, b], xall_ref.at[j, 4 + b], d_s.at[i], d_r.at[j], to_pt)

    def norm(j):
        arrived(raw_block(j, yo), raw_r.at[j % RSLOTS, 1])
        loads = [pltpu.make_async_copy(raw_block(j, b), lr.at[i], l_s.at[i]) for i, b in enumerate((yp, ym, yo))]
        for cp in loads:
            cp.start()
        for cp in loads:
            cp.wait()
        rows = pl.ds(pl.multiple_of(j * r, r), r)
        blocks = [(y, lambda: xr[rows]), (yp, lambda: lr[0]), (ym, lambda: lr[1]), (yo, lambda: lr[2])]
        total = jnp.zeros((r, 1), F32)
        for _, get in blocks:
            total += jnp.sum(get().astype(F32), axis=1, keepdims=True)
        mean = total / K
        total = jnp.zeros((r, 1), F32)
        for _, get in blocks:
            dev = get().astype(F32) - mean
            total += jnp.sum(dev * dev, axis=1, keepdims=True)
        inv = lax.rsqrt(total / K + LN_EPS)
        for b, get in blocks:
            ln[:, pl.ds(pl.multiple_of(b * KB, KB), KB)] = ((get().astype(F32) - mean) * inv * gv[b]).astype(BF16)
        out = pltpu.make_async_copy(ln, xall_ref.at[j, x], l_s.at[7])
        out.start()
        out.wait()
        x_own(j, to_xp, 0).start()
        x_own(j, to_xm, 1).start()
        d_copy(j, x, 0).start()

    def x_step(j):
        arrived(xall_ref.at[j, pl.ds(0, 2)], x_r.at[j, 0])
        x_relay(j, xm, 0, to_xp, 2).start()
        x_relay(j, xp, half, to_xm, 3).start()
        d_copy(j, xp, 1).start()
        d_copy(j, xm, 2).start()

    def x_last(j):
        arrived(xall_ref.at[j, xo], x_r.at[j, 1])
        d_copy(j, xo, 3).start()

    def raw_wait(j):
        arrived(raw_ref.at[pl.ds(0, 2), pl.ds(0, r)], raw_r.at[j % RSLOTS, 0])

    def raw_step(j):
        raw_wait(j)
        raw_relay(j, ym, 0, to_yp, 2).start()
        raw_relay(j, yp, half, to_ym, 3).start()

    def raw_tick(j):
        raw_step(j)

        send_raw(j + AHEAD)

        @pl.when(jnp.logical_and(j >= 3, j < J - AHEAD))
        def _():
            norm(j - 2)

    own_x.wait()
    own_g.wait()
    raw_wait(0)
    send_raw(AHEAD)
    arrived(gv.at[pl.ds(0, 3)], g_r)
    norm(0)
    loop(1, J - AHEAD, raw_tick)
    loop(J - AHEAD, J, raw_step)
    w1_sends = [w1_copy(b, dev, part) for part in (0, 1) for b, dev in ((yp, to_yp), (ym, to_ym), (yo, to_yo))]
    for cp in w1_sends:
        cp.start()
    loop(J - AHEAD - 2, J, norm)
    loop(0, J, x_step)
    loop(0, 3, x_last)

    def full(t):
        return (t, t, 0, r)

    def short(t):
        return (t, FULL + (t - FULL) // SPLIT, (t - FULL) % SPLIT * small, small)

    def x_load(k):
        t, j, off, n = k
        rows = pl.ds(0, n) if n == r else pl.ds(pl.multiple_of(off, small), n)
        return pltpu.make_async_copy(xall_ref.at[j, :, rows], xv.at[t % 2, :, pl.ds(0, n)], xl_s.at[t % 2])

    def x_fetch(k):
        arrived_rows = xall_ref.at[k[1], pl.ds(4, 4)]
        if k[3] == r:
            arrived(arrived_rows, d_r.at[k[1]])
        else:
            @pl.when(k[2] == 0)
            def _():
                arrived(arrived_rows, d_r.at[k[1]])
        x_load(k).start()

    x_fetch(full(0))
    own_w1.wait()
    own_w2.wait()
    w1_wait(0)

    def hcols(b, lo=0, hi=NS):
        return pl.ds(pl.multiple_of(b * NS + lo, 128), hi - lo)

    def h_own(k, dev, part):
        t, n = k[0], 8 * k[3]
        lo, hi = parts[part]
        blk = hv.at[t % HSLOTS, pl.ds(0, n), hcols(y, lo, hi)]
        return rc(blk, blk, h_s.at[t % HSLOTS], h_r.at[t % HSLOTS, 0], dev)

    def h_relay(k, b, side, dev):
        t, n = k[0], 4 * k[3]
        blk = hv.at[t % HSLOTS, pl.ds(side * n, n), hcols(b)]
        return rc(blk, blk, q_s.at[t % HSLOTS], h_r.at[t % HSLOTS, 1], dev)

    def h_bytes(k, blocks):
        return hv.at[k[0] % HSLOTS, pl.ds(0, 8 * k[3]), pl.ds(0, blocks * NS)]

    def sent(k):
        left(h_bytes(k, 2), h_s.at[k[0] % HSLOTS])
        left(h_bytes(k, 1), q_s.at[k[0] % HSLOTS])

    def start(k, fetch, first):
        t, n = k[0], k[3]
        x_load(k).wait()
        fetch()
        for part, (lo, hi) in enumerate(parts):
            if part == 1 and first is not None:
                @pl.when(first)
                def _():
                    w1_wait(1)
            rows = xv[t % 2, :, :n].reshape(8 * n, K)
            u = jnp.dot(rows, w1v[:, lo:hi], preferred_element_type=F32)
            hv[t % HSLOTS, :8 * n, hcols(y, lo, hi)] = jax.nn.gelu(u, approximate=True).astype(BF16)
            h_own(k, to_yp, part).start()
            h_own(k, to_ym, part).start()

    def relay(k):
        arrived(h_bytes(k, 2), h_r.at[k[0] % HSLOTS, 0])
        h_relay(k, ym, 0, to_yp).start()
        h_relay(k, yp, 1, to_ym).start()

    def p_copy(k):
        t, n = k[0], 4 * k[3]
        return rc(pv.at[t % 2, pl.ds(0, n)], pr.at[t % VSLOTS, pl.ds(0, n)], p_s.at[t % 2], p_r.at[t % VSLOTS], to_pt)

    def p_sent(k):
        p_copy(k).wait_send()

    def second(k):
        t, n = k[0], 4 * k[3]
        arrived(h_bytes(k, 1), h_r.at[t % HSLOTS, 1])
        tn = DB // 2

        def cols(i):
            o = pl.ds(pl.multiple_of(i * tn, tn), tn)
            u = jnp.dot(hv[t % HSLOTS, :2 * n], w2v[:, o], preferred_element_type=F32)
            sv[t % SSLOTS, :n, o] = u[:n]
            pv[t % 2, :n, o] = u[n:]
        loop(0, 2, cols)
        p_copy(k).start()

    def s_rows(k, b):
        return pl.ds(pl.multiple_of(b * k[3], k[3]), k[3])

    def f_copy(k, side, dev):
        t, n = k[0], k[3]
        cols = pl.ds(side * (DB // 2), DB // 2)
        return rc(sv.at[t % SSLOTS, s_rows(k, xo), cols], hr.at[t % FSLOTS, side, pl.ds(0, n)], f_s.at[t % SSLOTS], f_r.at[t % FSLOTS], dev)

    def t_copy(k, b, dev, q):
        t, n = k[0], k[3]
        return rc(sv.at[t % SSLOTS, s_rows(k, b)], tr.at[t % VSLOTS, q, pl.ds(0, n)], t_s.at[t % SSLOTS], t_r.at[t % VSLOTS], dev)

    def add_partner(k):
        t, n = k[0], 4 * k[3]
        p_copy(k).wait_recv()
        sv[t % SSLOTS, :n] += pr[t % VSLOTS, :n]
        f_copy(k, 0, to_xp).start()
        f_copy(k, 1, to_xm).start()

    def add_far(k):
        t, n = k[0], k[3]
        m = DB // 2
        arrived(hr.at[t % FSLOTS, :, pl.ds(0, n)], f_r.at[t % FSLOTS])
        sv[t % SSLOTS, s_rows(k, xp), :m] += hr[t % FSLOTS, 0, :n]
        sv[t % SSLOTS, s_rows(k, xm), m:] += hr[t % FSLOTS, 1, :n]
        t_copy(k, xp, to_xp, 1).start()
        t_copy(k, xm, to_xm, 0).start()

    def finish(k):
        t, j, off, n = k
        arrived(tr.at[t % VSLOTS, :, pl.ds(0, n)], t_r.at[t % VSLOTS])
        rows = pl.ds(pl.multiple_of(j * r + off, n), n)
        mlp = sv[t % SSLOTS, s_rows(k, x)] + tr[t % VSLOTS, 0, :n] + tr[t % VSLOTS, 1, :n]
        xr[rows] = (xr[rows].astype(F32) + mlp).astype(BF16)
        pltpu.make_async_copy(xr.at[rows], y_ref.at[rows], o_s).start()

    def s_sent(k):
        t, n = k[0], k[3]
        left(sv.at[t % SSLOTS, pl.ds(0, n)], f_s.at[t % SSLOTS])
        left(sv.at[t % SSLOTS, pl.ds(0, 2 * n)], t_s.at[t % SSLOTS])

    def tick(t):
        def when(lag, f, since=0):
            @pl.when(jnp.logical_and(t >= max(lag, since), t < FULL + lag))
            def _():
                f(full(t - lag))

            @pl.when(t >= FULL + lag)
            def _():
                f(short(t - lag))

        def begin(k):
            def fetch():
                if k[3] == r:
                    @pl.when(t + 1 < FULL)
                    def _():
                        x_fetch(full(t + 1))

                    @pl.when(t + 1 == FULL)
                    def _():
                        x_fetch(short(t + 1))
                else:
                    @pl.when(t + 1 < TICKS)
                    def _():
                        x_fetch(short(t + 1))
            start(k, fetch, t == 0 if k[3] == r else None)
        when(3, sent)
        when(0, begin)
        when(1, relay)
        when(3, add_partner)

        @pl.when(t + 3 < J)
        def _():
            x_last(t + 3)
        when(4, p_sent)
        when(2, second)

        @pl.when(jnp.logical_and(t >= 4, t <= CATCH))
        def _():
            add_far(full(t - 4))
        when(3, add_far, CATCH)

        @pl.when(jnp.logical_and(t >= 5, t <= CATCH + 1))
        def _():
            finish(full(t - 5))
        when(4, finish, CATCH + 1)
        when(5, s_sent)
    loop(0, TICKS, tick)

    n4, n3, n2, n1 = (short(TICKS - i) for i in (4, 3, 2, 1))
    n5 = full(TICKS - 5)
    relay(n1)
    add_partner(n3)
    p_sent(n4)
    second(n2)
    add_far(n3)
    p_sent(n3)
    s_sent(n5)
    second(n1)
    add_partner(n2)
    finish(n4)
    add_partner(n1)
    add_far(n2)
    finish(n3)
    add_far(n1)
    finish(n2)
    finish(n1)
    for k in (n3, n2, n1):
        sent(k)
    p_sent(n2)
    p_sent(n1)
    for k in (n4, n3, n2, n1):
        s_sent(k)

    left(gv.at[pl.ds(0, 3)], g_s)
    for part, (lo, hi) in enumerate(parts):
        left(w1v.at[pl.ds(0, 3 * KB), pl.ds(lo, hi - lo)], w1_s.at[part])
    left(x_ref, raw_s.at[0])
    left(x_ref, raw_s.at[1])
    rest = pl.ds(0, (J - 1) * half)
    left(x_ref.at[rest], raw_s.at[2])
    left(x_ref.at[rest], raw_s.at[3])
    left(x_ref.at[pl.ds(0, r)], raw_s.at[4])
    for i in (0, 1):
        left(xall_ref.at[pl.ds(0, J // 8)], x_s.at[i])
    for i in (2, 3):
        left(xall_ref.at[pl.ds(0, J // 16)], x_s.at[i])
    for i in range(4):
        left(xall_ref.at[pl.ds(0, J // 8)], d_s.at[i])
    pltpu.make_async_copy(xr, y_ref, o_s).wait()


def solution(mesh):
    assert mesh.shape["tp2"] == RING and mesh.shape["tp"] == 2 * RING
    row_spec = P(("data", "tp"), "tp2")

    def local_block(x_loc, scale_loc, w_in_loc, w_out_loc):
        T, KB = x_loc.shape
        NB, DB = w_out_loc.shape
        NS, K, r = NB // RING, RING * KB, T // CHUNKS
        dma = pltpu.SemaphoreType.DMA
        any_spec = pl.BlockSpec(memory_space=pl.ANY)
        outs = pl.pallas_call(
            functools.partial(kernel, (T, KB, NS, DB, r)),
            out_shape=[
                jax.ShapeDtypeStruct((T, DB), BF16),
                jax.ShapeDtypeStruct((RING, T, KB), BF16),
                jax.ShapeDtypeStruct((CHUNKS, 8, r, K), BF16),
            ],
            in_specs=[any_spec] * 4,
            out_specs=[any_spec] * 3,
            scratch_shapes=[
                pltpu.VMEM((K, NS), BF16),
                pltpu.VMEM((NB, DB), BF16),
                pltpu.VMEM((2, 8, r, K), BF16),
                pltpu.VMEM((HSLOTS, 8 * r, NB), BF16),
                pltpu.VMEM((SSLOTS, 4 * r, DB), F32),
                pltpu.VMEM((2, 4 * r, DB), F32),
                pltpu.VMEM((VSLOTS, 4 * r, DB), F32),
                pltpu.VMEM((FSLOTS, 2, r, DB // 2), F32),
                pltpu.VMEM((VSLOTS, 2, r, DB), F32),
                pltpu.VMEM((T, DB), BF16),
                pltpu.VMEM((RING, 1, KB), F32),
                pltpu.VMEM((3, r, KB), BF16),
                pltpu.VMEM((r, K), BF16),
                dma, dma,
                dma((5,)), dma((RSLOTS, 2)),
                dma((2,)), dma((2,)),
                dma((4,)), dma((CHUNKS, 2)),
                dma((4,)), dma((CHUNKS,)),
                dma((HSLOTS,)), dma((HSLOTS, 2)), dma((HSLOTS,)),
                dma((2,)), dma((VSLOTS,)),
                dma((SSLOTS,)), dma((FSLOTS,)),
                dma((SSLOTS,)), dma((VSLOTS,)),
                dma((8,)), dma((2,)), dma,
            ],
            compiler_params=pltpu.CompilerParams(collective_id=0, has_side_effects=True, vmem_limit_bytes=67043328),
        )(x_loc, scale_loc.reshape(1, KB), w_in_loc, w_out_loc)
        return outs[0]

    return jax.shard_map(local_block, mesh=mesh, in_specs=(row_spec, P("tp2"), P("tp2", "tp"), P("tp", "tp2")), out_specs=row_spec, check_vma=False)
```

time: 1180 us -> 495 us (0.42)
  waiting for transfers between devices: 993 us -> 0 us
  Pallas kernels: 0 us -> 490 us
  matrix products: 142 us -> 0 us
  other arithmetic: 20.2 us -> 0 us
  between operations: 13.2 us -> 0.01 us
    reduce_scatter x2 -> x0, waiting for transfers between devices: 652 us -> none  [the longest x1 483 us: local_block(): pre_act = lax.psum_scatter(part_pre, 'tp2', scatter_dimension=0, tiled=True)]
    pallas_call x0 -> x1, Pallas kernels: none -> 490 us  [local_block(): pl.pallas_call(functools.partial(kernel, (T, KB, NS, DB, r)), out_shape=[...]
    all_gather x2 -> x0, waiting for transfers between devices: 341 us -> none  [the longest x1 256 us: local_block(): hidden_all = lax.all_gather(hidden, 'tp2', axis=0, tiled=True)]
    dot_general x2 -> x0, matrix products: 142 us -> none  [the longest x1 71.2 us: local_block(): part_pre = jnp.dot(x_group, w_in_loc, preferred_element_type=jnp.float32)]
    convert_element_type x3 -> x0, other arithmetic: 17.9 us -> none  [the longest x1 10.1 us: local_block(): hidden = jax.nn.gelu(pre_act, approximate=True).astype(jnp.bfloat16)]
  transfers between devices with their start and end apart: 4 -> 0, of which waited for: 4 -> 0; matrix products, arithmetic and copies ran while one was open for 0% -> 0% of each run, Pallas kernels for 0% -> 0%
where the time goes in v2:
time: 495 us; the launch traced here: 494 us
  Pallas kernels  490 us (99%)
    pallas_call x1, Pallas kernels, local_block(): pl.pallas_call(functools.partial(kernel, (T, KB, NS, DB, r)), out_shape=[...  490 us

profile of v2, /device:TPU:97, one launch (start us, length us, event | category | flops | bytes accessed | tf_op | source)
XLA Modules:
  0.0 493.6 jit_solution(2898188057443839992)
XLA Ops:
  0.0 490.4 %shard_map.46 = (bf16[512,2048]{1,0:T(8,128)(2,1)}, bf16[4,512,2048]{2,1,0:T(8,128)(2,1)}, bf16[16,8,32,8192]{3,2,1,0:T(8,128)(2,1)}) custom-call(bf16[512,2048]{1,0:T(8,128)(2,1)} %x_ref.1, f32[1,2048]{1,0:T(1,128)} %bitcast.1, bf16[2048,3584]{1,0:T(8,128)(2,1)} %w1_ref.1, bf16[3584,2048]{1,0:T(8,128)(2,1)} %w2_ref.1), custom_call_target="tpu_custom_call" | custom-call | tf_op jit(solution)/shard_map/pallas_call | solution.py:415
  490.4 3.2 copy.6

commit v3 on v2

--- a/solution.py
+++ b/solution.py
@@ -10,7 +10,7 @@
 LN_EPS = 1e-6
 RING = 4
 CHUNKS = 16
-FULL = 14
+FULL = 12
 SPLIT = 2
 TICKS = FULL + (CHUNKS - FULL) * SPLIT
 AHEAD = 4
@@ -20,7 +20,7 @@
 BF16, F32 = jnp.bfloat16, jnp.float32
 
 
-def kernel(dims, x_ref, g_ref, w1_ref, w2_ref, y_ref, raw_ref, xall_ref, w1v, w2v, xv, hv, sv, pv, pr, hr, tr, xr, gv, lr, ln,
+def kernel(dims, x_ref, g_ref, w1_ref, w2_ref, xr, raw_ref, xall_ref, w1v, w2v, xv, hv, sv, pv, pr, hr, tr, gv, lr, ln,
            g_s, g_r, raw_s, raw_r, w1_s, w1_r, x_s, x_r, d_s, d_r, h_s, h_r, q_s, p_s, p_r, f_s, f_r, t_s, t_r, l_s, xl_s, o_s):
     T, KB, NS, DB, r = dims
     J, K, small = CHUNKS, RING * KB, r // SPLIT
@@ -270,6 +270,29 @@
         loop(0, 2, cols)
         p_copy(k).start()
 
+    def second_part(k, blocks, add):
+        t, n = k[0], 4 * k[3]
+        tn = DB // 2
+
+        def cols(i):
+            o = pl.ds(pl.multiple_of(i * tn, tn), tn)
+            u = sum(jnp.dot(hv[t % HSLOTS, :2 * n, hcols(b)], w2v[pl.ds(pl.multiple_of(b * NS, NS), NS), o], preferred_element_type=F32) for b in blocks)
+            if add:
+                sv[t % SSLOTS, :n, o] += u[:n]
+                pv[t % 2, :n, o] += u[n:]
+            else:
+                sv[t % SSLOTS, :n, o] = u[:n]
+                pv[t % 2, :n, o] = u[n:]
+        loop(0, 2, cols)
+
+    def second_early(k):
+        second_part(k, (y, yp, ym), False)
+
+    def second_late(k):
+        arrived(h_bytes(k, 1), h_r.at[k[0] % HSLOTS, 1])
+        second_part(k, (yo,), True)
+        p_copy(k).start()
+
     def s_rows(k, b):
         return pl.ds(pl.multiple_of(b * k[3], k[3]), k[3])
 
@@ -304,7 +327,6 @@
         rows = pl.ds(pl.multiple_of(j * r + off, n), n)
         mlp = sv[t % SSLOTS, s_rows(k, x)] + tr[t % VSLOTS, 0, :n] + tr[t % VSLOTS, 1, :n]
         xr[rows] = (xr[rows].astype(F32) + mlp).astype(BF16)
-        pltpu.make_async_copy(xr.at[rows], y_ref.at[rows], o_s).start()
 
     def s_sent(k):
         t, n = k[0], k[3]
@@ -312,8 +334,8 @@
         left(sv.at[t % SSLOTS, pl.ds(0, 2 * n)], t_s.at[t % SSLOTS])
 
     def tick(t):
-        def when(lag, f, since=0):
-            @pl.when(jnp.logical_and(t >= max(lag, since), t < FULL + lag))
+        def when(lag, f):
+            @pl.when(jnp.logical_and(t >= lag, t < FULL + lag))
             def _():
                 f(full(t - lag))
 
@@ -339,6 +361,14 @@
         when(3, sent)
         when(0, begin)
         when(1, relay)
+
+        @pl.when(t == FULL + 3)
+        def _():
+            add_far(full(t - 4))
+
+        @pl.when(t > FULL + 3)
+        def _():
+            add_far(short(t - 4))
         when(3, add_partner)
 
         @pl.when(t + 3 < J)
@@ -350,26 +380,29 @@
         @pl.when(jnp.logical_and(t >= 4, t <= CATCH))
         def _():
             add_far(full(t - 4))
-        when(3, add_far, CATCH)
-
-        @pl.when(jnp.logical_and(t >= 5, t <= CATCH + 1))
-        def _():
-            finish(full(t - 5))
-        when(4, finish, CATCH + 1)
+
+        @pl.when(jnp.logical_and(t >= CATCH, t < FULL + 2))
+        def _():
+            add_far(full(t - 3))
+        when(5, finish)
         when(5, s_sent)
     loop(0, TICKS, tick)
 
     n4, n3, n2, n1 = (short(TICKS - i) for i in (4, 3, 2, 1))
-    n5 = full(TICKS - 5)
+    n5 = short(TICKS - 5)
+    add_partner(n3)
+    add_far(n4)
+    p_sent(n4)
     relay(n1)
-    add_partner(n3)
-    p_sent(n4)
-    second(n2)
+    second_early(n2)
+    second_late(n2)
+    p_sent(n3)
+    finish(n5)
+    s_sent(n5)
     add_far(n3)
-    p_sent(n3)
-    s_sent(n5)
-    second(n1)
+    second_early(n1)
     add_partner(n2)
+    second_late(n1)
     finish(n4)
     add_partner(n1)
     add_far(n2)
@@ -399,7 +432,6 @@
         left(xall_ref.at[pl.ds(0, J // 16)], x_s.at[i])
     for i in range(4):
         left(xall_ref.at[pl.ds(0, J // 8)], d_s.at[i])
-    pltpu.make_async_copy(xr, y_ref, o_s).wait()
 
 
 def solution(mesh):
@@ -415,12 +447,12 @@
         outs = pl.pallas_call(
             functools.partial(kernel, (T, KB, NS, DB, r)),
             out_shape=[
-                jax.ShapeDtypeStruct((T, DB), BF16),
+                pltpu.VMEM((T, DB), BF16),
                 jax.ShapeDtypeStruct((RING, T, KB), BF16),
                 jax.ShapeDtypeStruct((CHUNKS, 8, r, K), BF16),
             ],
             in_specs=[any_spec] * 4,
-            out_specs=[any_spec] * 3,
+            out_specs=[pl.BlockSpec(memory_space=pltpu.VMEM), any_spec, any_spec],
             scratch_shapes=[
                 pltpu.VMEM((K, NS), BF16),
                 pltpu.VMEM((NB, DB), BF16),
@@ -431,7 +463,6 @@
                 pltpu.VMEM((VSLOTS, 4 * r, DB), F32),
                 pltpu.VMEM((FSLOTS, 2, r, DB // 2), F32),
                 pltpu.VMEM((VSLOTS, 2, r, DB), F32),
-                pltpu.VMEM((T, DB), BF16),
                 pltpu.VMEM((RING, 1, KB), F32),
                 pltpu.VMEM((3, r, KB), BF16),
                 pltpu.VMEM((r, K), BF16),
@@ -446,7 +477,7 @@
                 dma((SSLOTS,)), dma((VSLOTS,)),
                 dma((8,)), dma((2,)), dma,
             ],
-            compiler_params=pltpu.CompilerParams(collective_id=0, has_side_effects=True, vmem_limit_bytes=67043328),
+            compiler_params=pltpu.CompilerParams(collective_id=0, has_side_effects=True, vmem_limit_bytes=60 * 2**20),
         )(x_loc, scale_loc.reshape(1, KB), w_in_loc, w_out_loc)
         return outs[0]
 

time: 495 us -> 489 us (0.988)
  no operation moved by 1% of the time
where the time goes in v3:
time: 489 us
  Pallas kernels  487 us (100%)
    pallas_call x1, Pallas kernels, local_block(): pl.pallas_call(functools.partial(kernel, (T, KB, NS, DB, r)), out_shape=[...  487 us

profile of v3, /device:TPU:97, one launch (start us, length us, event | category | flops | bytes accessed | tf_op | source)
XLA Modules:
  0.0 488.6 jit_solution(18314976946753595755)
XLA Ops:
  0.0 487.2 %shard_map.46 = (bf16[512,2048]{1,0:T(8,128)(2,1)S(1)}, bf16[4,512,2048]{2,1,0:T(8,128)(2,1)}, bf16[16,8,32,8192]{3,2,1,0:T(8,128)(2,1)}) custom-call(bf16[512,2048]{1,0:T(8,128)(2,1)} %x_ref.1, f32[1,2048]{1,0:T(1,128)} %bitcast.1, bf16[2048,3584]{1,0:T(8,128)(2,1)} %w1_ref.1, bf16[3584,2048]{1,0:T(8,128)(2,1)} %w2_ref.1), custom_call_target="tpu_custom_call" | custom-call | tf_op jit(solution)/shard_map/pallas_call | solution.py:447
  487.2 1.3 copy.6

commit v4 on v3

--- a/solution.py
+++ b/solution.py
@@ -13,15 +13,16 @@
 FULL = 12
 SPLIT = 2
 TICKS = FULL + (CHUNKS - FULL) * SPLIT
+FAR, NEAR, OWN = FULL, FULL + 2, FULL + 6
 AHEAD = 4
 CATCH = 8
-RSLOTS, HSLOTS, SSLOTS, VSLOTS, FSLOTS = 8, 5, 4, 3, 4
+RSLOTS, HSLOTS, SSLOTS, PSLOTS, VSLOTS, FSLOTS = 8, 5, 4, 2, 3, 4
 MESH = pl.DeviceIdType.MESH
 BF16, F32 = jnp.bfloat16, jnp.float32
 
 
-def kernel(dims, x_ref, g_ref, w1_ref, w2_ref, xr, raw_ref, xall_ref, w1v, w2v, xv, hv, sv, pv, pr, hr, tr, gv, lr, ln,
-           g_s, g_r, raw_s, raw_r, w1_s, w1_r, x_s, x_r, d_s, d_r, h_s, h_r, q_s, p_s, p_r, f_s, f_r, t_s, t_r, l_s, xl_s, o_s):
+def kernel(dims, x_ref, g_ref, w1_ref, w2_ref, xr, raw_ref, xall_ref, w1v, w2v, xv, hv, sv, pv, pr, hr, tr, hx, tx, gv,
+           g_s, g_r, raw_s, raw_r, w1_s, w1_r, x_s, x_r, d_s, d_r, h_s, h_r, q_s, p_s, p_r, f_s, f_r, t_s, t_r, tx_r, l_s, xl_s, o_s):
     T, KB, NS, DB, r = dims
     J, K, small = CHUNKS, RING * KB, r // SPLIT
     half = r // 2
@@ -115,13 +116,13 @@
 
     def norm(j):
         arrived(raw_block(j, yo), raw_r.at[j % RSLOTS, 1])
-        loads = [pltpu.make_async_copy(raw_block(j, b), lr.at[i], l_s.at[i]) for i, b in enumerate((yp, ym, yo))]
+        loads = [pltpu.make_async_copy(raw_block(j, b), xv.at[1, 1 + i, :, pl.ds(0, KB)], l_s.at[i]) for i, b in enumerate((yp, ym, yo))]
         for cp in loads:
             cp.start()
         for cp in loads:
             cp.wait()
         rows = pl.ds(pl.multiple_of(j * r, r), r)
-        blocks = [(y, lambda: xr[rows]), (yp, lambda: lr[0]), (ym, lambda: lr[1]), (yo, lambda: lr[2])]
+        blocks = [(y, lambda: xr[rows]), (yp, lambda: xv[1, 1, :, :KB]), (ym, lambda: xv[1, 2, :, :KB]), (yo, lambda: xv[1, 3, :, :KB])]
         total = jnp.zeros((r, 1), F32)
         for _, get in blocks:
             total += jnp.sum(get().astype(F32), axis=1, keepdims=True)
@@ -132,8 +133,8 @@
             total += jnp.sum(dev * dev, axis=1, keepdims=True)
         inv = lax.rsqrt(total / K + LN_EPS)
         for b, get in blocks:
-            ln[:, pl.ds(pl.multiple_of(b * KB, KB), KB)] = ((get().astype(F32) - mean) * inv * gv[b]).astype(BF16)
-        out = pltpu.make_async_copy(ln, xall_ref.at[j, x], l_s.at[7])
+            xv[1, 0, :, pl.ds(pl.multiple_of(b * KB, KB), KB)] = ((get().astype(F32) - mean) * inv * gv[b]).astype(BF16)
+        out = pltpu.make_async_copy(xv.at[1, 0], xall_ref.at[j, x], l_s.at[7])
         out.start()
         out.wait()
         x_own(j, to_xp, 0).start()
@@ -181,7 +182,7 @@
         cp.start()
     loop(J - AHEAD - 2, J, norm)
     loop(0, J, x_step)
-    loop(0, 3, x_last)
+    loop(0, 4, x_last)
 
     def full(t):
         return (t, t, 0, r)
@@ -190,21 +191,44 @@
         return (t, FULL + (t - FULL) // SPLIT, (t - FULL) % SPLIT * small, small)
 
     def x_load(k):
-        t, j, off, n = k
-        rows = pl.ds(0, n) if n == r else pl.ds(pl.multiple_of(off, small), n)
-        return pltpu.make_async_copy(xall_ref.at[j, :, rows], xv.at[t % 2, :, pl.ds(0, n)], xl_s.at[t % 2])
-
-    def x_fetch(k):
-        arrived_rows = xall_ref.at[k[1], pl.ds(4, 4)]
+        t, j = k[:2]
+        return pltpu.make_async_copy(xall_ref.at[j], xv.at[t % 2], xl_s.at[t % 2])
+
+    def x_piece(t, j, b, rows, i, to):
+        pltpu.make_async_copy(xall_ref.at[j, b, rows], xv.at[t % 2, i, to], xl_s.at[t % 2]).start()
+
+    def x_loaded(k):
         if k[3] == r:
-            arrived(arrived_rows, d_r.at[k[1]])
+            x_load(k).wait()
         else:
-            @pl.when(k[2] == 0)
+            half_slot = xv.at[k[0] % 2, pl.ds(0, 4)]
+            pltpu.make_async_copy(xall_ref.at[0, pl.ds(0, 4)], half_slot, xl_s.at[k[0] % 2]).wait()
+
+    def gathered(j):
+        arrived(xall_ref.at[j, pl.ds(4, 4)], d_r.at[j])
+
+    def fetch_full(t):
+        gathered(t)
+        x_load(full(t)).start()
+
+    def fetch_owner(t):
+        for i in (0, 1):
+            @pl.when(t == FAR + i)
             def _():
-                arrived(arrived_rows, d_r.at[k[1]])
-        x_load(k).start()
-
-    x_fetch(full(0))
+                gathered(FULL + 2 * i)
+                gathered(FULL + 2 * i + 1)
+        every = pl.ds(0, r)
+        order = {FAR + i: ((FULL + 2 * i, xo), (FULL + 2 * i + 1, xo)) for i in (0, 1)}
+        order |= {NEAR + i: ((FULL + i, xp), (FULL + i, xm)) for i in range(4)}
+        order |= {OWN + i: ((FULL + 2 * i, x), (FULL + 2 * i + 1, x)) for i in (0, 1)}
+        for which, blocks in order.items():
+            @pl.when(t == which)
+            def _():
+                for i, (j, b) in enumerate(blocks):
+                    x_piece(t, j, b, every, i, every)
+                    x_piece(t, j, 4 + b, every, 2 + i, every)
+
+    fetch_full(0)
     own_w1.wait()
     own_w2.wait()
     w1_wait(0)
@@ -232,14 +256,14 @@
 
     def start(k, fetch, first):
         t, n = k[0], k[3]
-        x_load(k).wait()
+        x_loaded(k)
         fetch()
         for part, (lo, hi) in enumerate(parts):
             if part == 1 and first is not None:
                 @pl.when(first)
                 def _():
                     w1_wait(1)
-            rows = xv[t % 2, :, :n].reshape(8 * n, K)
+            rows = xv[t % 2, :8 * n // r].reshape(8 * n, K)
             u = jnp.dot(rows, w1v[:, lo:hi], preferred_element_type=F32)
             hv[t % HSLOTS, :8 * n, hcols(y, lo, hi)] = jax.nn.gelu(u, approximate=True).astype(BF16)
             h_own(k, to_yp, part).start()
@@ -252,7 +276,7 @@
 
     def p_copy(k):
         t, n = k[0], 4 * k[3]
-        return rc(pv.at[t % 2, pl.ds(0, n)], pr.at[t % VSLOTS, pl.ds(0, n)], p_s.at[t % 2], p_r.at[t % VSLOTS], to_pt)
+        return rc(pv.at[t % 2, pl.ds(0, n)], pr.at[t % PSLOTS, pl.ds(0, n)], p_s.at[t % 2], p_r.at[t % PSLOTS], to_pt)
 
     def p_sent(k):
         p_copy(k).wait_send()
@@ -305,10 +329,13 @@
         t, n = k[0], k[3]
         return rc(sv.at[t % SSLOTS, s_rows(k, b)], tr.at[t % VSLOTS, q, pl.ds(0, n)], t_s.at[t % SSLOTS], t_r.at[t % VSLOTS], dev)
 
-    def add_partner(k):
+    def add_core(k):
         t, n = k[0], 4 * k[3]
         p_copy(k).wait_recv()
-        sv[t % SSLOTS, :n] += pr[t % VSLOTS, :n]
+        sv[t % SSLOTS, :n] += pr[t % PSLOTS, :n]
+
+    def add_partner(k):
+        add_core(k)
         f_copy(k, 0, to_xp).start()
         f_copy(k, 1, to_xm).start()
 
@@ -333,47 +360,85 @@
         left(sv.at[t % SSLOTS, pl.ds(0, n)], f_s.at[t % SSLOTS])
         left(sv.at[t % SSLOTS, pl.ds(0, 2 * n)], t_s.at[t % SSLOTS])
 
+    def send_far(i):
+        t = FAR + i
+        add_core(short(t))
+        for side, dev in ((0, to_xp), (1, to_xm)):
+            src = sv.at[t % SSLOTS, pl.ds(0, 2 * r), pl.ds(side * (DB // 2), DB // 2)]
+            rc(src, hx.at[i, side], f_s.at[t % SSLOTS], f_r.at[t % FSLOTS], dev).start()
+
+    def send_near(i):
+        t = NEAR + i
+        add_core(short(t))
+        if i % 2 == 0:
+            arrived(hx.at[i // 2], f_r.at[(FAR + i // 2) % FSLOTS])
+        m, slot, rows = DB // 2, t % SSLOTS, pl.ds(i % 2 * r, r)
+        sv[slot, :r, :m] += hx[i // 2, 0, rows]
+        sv[slot, r:2 * r, m:] += hx[i // 2, 1, rows]
+        rc(sv.at[slot, pl.ds(0, r)], tx.at[i, 1], t_s.at[slot], tx_r.at[i], to_xp).start()
+        rc(sv.at[slot, pl.ds(r, r)], tx.at[i, 0], t_s.at[slot], tx_r.at[i], to_xm).start()
+
+    def finish_own(i):
+        t = OWN + i
+        for h in (0, 1):
+            q = 2 * i + h
+            arrived(tx.at[q], tx_r.at[q])
+            rows = pl.ds((FULL + q) * r, r)
+            mlp = sv[t % SSLOTS, h * r:(h + 1) * r] + tx[q, 0] + tx[q, 1]
+            xr[rows] = (xr[rows].astype(F32) + mlp).astype(BF16)
+
+    def two_rows_left(sem):
+        left(sv.at[0, pl.ds(0, 2 * r)], sem)
+
     def tick(t):
-        def when(lag, f):
+        def when(lag, f, until=TICKS):
             @pl.when(jnp.logical_and(t >= lag, t < FULL + lag))
             def _():
                 f(full(t - lag))
 
-            @pl.when(t >= FULL + lag)
-            def _():
-                f(short(t - lag))
+            if until > FULL:
+                @pl.when(jnp.logical_and(t >= FULL + lag, t < until + lag))
+                def _():
+                    f(short(t - lag))
 
         def begin(k):
             def fetch():
                 if k[3] == r:
                     @pl.when(t + 1 < FULL)
                     def _():
-                        x_fetch(full(t + 1))
+                        fetch_full(t + 1)
 
                     @pl.when(t + 1 == FULL)
                     def _():
-                        x_fetch(short(t + 1))
+                        fetch_owner(t + 1)
                 else:
                     @pl.when(t + 1 < TICKS)
                     def _():
-                        x_fetch(short(t + 1))
+                        fetch_owner(t + 1)
             start(k, fetch, t == 0 if k[3] == r else None)
         when(3, sent)
         when(0, begin)
         when(1, relay)
 
+        for i in (0, 1):
+            @pl.when(t == FAR + i + 3)
+            def _():
+                send_far(i)
+
+        for i in (0, 1, 2):
+            @pl.when(t == NEAR + i + 3)
+            def _():
+                send_near(i)
+
         @pl.when(t == FULL + 3)
         def _():
             add_far(full(t - 4))
 
-        @pl.when(t > FULL + 3)
+        when(3, add_partner, FULL)
+
+        @pl.when(t + 4 < J)
         def _():
-            add_far(short(t - 4))
-        when(3, add_partner)
-
-        @pl.when(t + 3 < J)
-        def _():
-            x_last(t + 3)
+            x_last(t + 4)
         when(4, p_sent)
         when(2, second)
 
@@ -384,38 +449,36 @@
         @pl.when(jnp.logical_and(t >= CATCH, t < FULL + 2))
         def _():
             add_far(full(t - 3))
-        when(5, finish)
-        when(5, s_sent)
+        when(5, finish, FULL)
+        when(5, s_sent, FULL)
+
+        for i in (0, 1):
+            @pl.when(t == FAR + i + 5)
+            def _():
+                two_rows_left(f_s.at[(FAR + i) % SSLOTS])
     loop(0, TICKS, tick)
 
     n4, n3, n2, n1 = (short(TICKS - i) for i in (4, 3, 2, 1))
-    n5 = short(TICKS - 5)
-    add_partner(n3)
-    add_far(n4)
+    send_near(3)
     p_sent(n4)
+    two_rows_left(t_s.at[NEAR % SSLOTS])
     relay(n1)
     second_early(n2)
     second_late(n2)
     p_sent(n3)
-    finish(n5)
-    s_sent(n5)
-    add_far(n3)
+    two_rows_left(t_s.at[(NEAR + 1) % SSLOTS])
     second_early(n1)
-    add_partner(n2)
+    add_core(n2)
     second_late(n1)
-    finish(n4)
-    add_partner(n1)
-    add_far(n2)
-    finish(n3)
-    add_far(n1)
-    finish(n2)
-    finish(n1)
+    finish_own(0)
+    add_core(n1)
+    finish_own(1)
     for k in (n3, n2, n1):
         sent(k)
     p_sent(n2)
     p_sent(n1)
-    for k in (n4, n3, n2, n1):
-        s_sent(k)
+    two_rows_left(t_s.at[(NEAR + 2) % SSLOTS])
+    two_rows_left(t_s.at[(NEAR + 3) % SSLOTS])
 
     left(gv.at[pl.ds(0, 3)], g_s)
     for part, (lo, hi) in enumerate(parts):
@@ -460,24 +523,24 @@
                 pltpu.VMEM((HSLOTS, 8 * r, NB), BF16),
                 pltpu.VMEM((SSLOTS, 4 * r, DB), F32),
                 pltpu.VMEM((2, 4 * r, DB), F32),
-                pltpu.VMEM((VSLOTS, 4 * r, DB), F32),
+                pltpu.VMEM((PSLOTS, 4 * r, DB), F32),
                 pltpu.VMEM((FSLOTS, 2, r, DB // 2), F32),
                 pltpu.VMEM((VSLOTS, 2, r, DB), F32),
+                pltpu.VMEM((2, 2, 2 * r, DB // 2), F32),
+                pltpu.VMEM((4, 2, r, DB), F32),
                 pltpu.VMEM((RING, 1, KB), F32),
-                pltpu.VMEM((3, r, KB), BF16),
-                pltpu.VMEM((r, K), BF16),
                 dma, dma,
                 dma((5,)), dma((RSLOTS, 2)),
                 dma((2,)), dma((2,)),
                 dma((4,)), dma((CHUNKS, 2)),
                 dma((4,)), dma((CHUNKS,)),
                 dma((HSLOTS,)), dma((HSLOTS, 2)), dma((HSLOTS,)),
-                dma((2,)), dma((VSLOTS,)),
+                dma((2,)), dma((PSLOTS,)),
                 dma((SSLOTS,)), dma((FSLOTS,)),
-                dma((SSLOTS,)), dma((VSLOTS,)),
+                dma((SSLOTS,)), dma((VSLOTS,)), dma((4,)),
                 dma((8,)), dma((2,)), dma,
             ],
-            compiler_params=pltpu.CompilerParams(collective_id=0, has_side_effects=True, vmem_limit_bytes=60 * 2**20),
+            compiler_params=pltpu.CompilerParams(collective_id=0, has_side_effects=True, vmem_limit_bytes=61 * 2**20 + 3 * 2**18),
         )(x_loc, scale_loc.reshape(1, KB), w_in_loc, w_out_loc)
         return outs[0]
 

time: 489 us -> 480 us (0.982)
  Pallas kernels: 487 us -> 478 us
    pallas_call x1, Pallas kernels: 487 us -> 478 us  [local_block(): pl.pallas_call(functools.partial(kernel, (T, KB, NS, DB, r)), out_shape=[...]
where the time goes in v4:
time: 480 us
  Pallas kernels  478 us (100%)
    pallas_call x1, Pallas kernels, local_block(): pl.pallas_call(functools.partial(kernel, (T, KB, NS, DB, r)), out_shape=[...  478 us

profile of v4, /device:TPU:97, one launch (start us, length us, event | category | flops | bytes accessed | tf_op | source)
XLA Modules:
  0.0 479.5 jit_solution(4585416669374535349)
XLA Ops:
  0.0 478.2 %shard_map.46 = (bf16[512,2048]{1,0:T(8,128)(2,1)S(1)}, bf16[4,512,2048]{2,1,0:T(8,128)(2,1)}, bf16[16,8,32,8192]{3,2,1,0:T(8,128)(2,1)}) custom-call(bf16[512,2048]{1,0:T(8,128)(2,1)} %x_ref.1, f32[1,2048]{1,0:T(1,128)} %bitcast.1, bf16[2048,3584]{1,0:T(8,128)(2,1)} %w1_ref.1, bf16[3584,2048]{1,0:T(8,128)(2,1)} %w2_ref.1), custom_call_target="tpu_custom_call" | custom-call | tf_op jit(solution)/shard_map/pallas_call | solution.py:510
  478.2 1.3 copy.6

commit v5 on v4

--- a/solution.py
+++ b/solution.py
@@ -304,6 +304,7 @@
             if add:
                 sv[t % SSLOTS, :n, o] += u[:n]
                 pv[t % 2, :n, o] += u[n:]
+                rc(pv.at[t % 2, pl.ds(0, n), o], pr.at[t % PSLOTS, pl.ds(0, n), o], p_s.at[t % 2], p_r.at[t % PSLOTS], to_pt).start()
             else:
                 sv[t % SSLOTS, :n, o] = u[:n]
                 pv[t % 2, :n, o] = u[n:]
@@ -315,7 +316,6 @@
     def second_late(k):
         arrived(h_bytes(k, 1), h_r.at[k[0] % HSLOTS, 1])
         second_part(k, (yo,), True)
-        p_copy(k).start()
 
     def s_rows(k, b):
         return pl.ds(pl.multiple_of(b * k[3], k[3]), k[3])

time: 480 us -> 480 us (level)
  no operation moved by 1% of the time
where the time goes in v5:
time: 480 us; the launch traced here: 479 us
  Pallas kernels  478 us (100%)
    pallas_call x1, Pallas kernels, local_block(): pl.pallas_call(functools.partial(kernel, (T, KB, NS, DB, r)), out_shape=[...  478 us

profile of v5, /device:TPU:97, one launch (start us, length us, event | category | flops | bytes accessed | tf_op | source)
XLA Modules:
  0.0 479.1 jit_solution(2170312449199567652)
XLA Ops:
  0.0 477.8 %shard_map.46 = (bf16[512,2048]{1,0:T(8,128)(2,1)S(1)}, bf16[4,512,2048]{2,1,0:T(8,128)(2,1)}, bf16[16,8,32,8192]{3,2,1,0:T(8,128)(2,1)}) custom-call(bf16[512,2048]{1,0:T(8,128)(2,1)} %x_ref.1, f32[1,2048]{1,0:T(1,128)} %bitcast.1, bf16[2048,3584]{1,0:T(8,128)(2,1)} %w1_ref.1, bf16[3584,2048]{1,0:T(8,128)(2,1)} %w2_ref.1), custom_call_target="tpu_custom_call" | custom-call | tf_op jit(solution)/shard_map/pallas_call | solution.py:510
  477.8 1.3 copy.6
